TPU v7x, 32 devices: a whole 2x2x4 slice. The times are simulated.
32 devices in a mesh: band: 4 (over y, core), tile: 8 (over z, x).
Axes of the slice: x: 2, y: 2, z: 4, core: 2. Of those that a mesh axis runs over, the one named last changes fastest.
Arguments:
- patches: bfloat16 [262144, 128], P(('band', 'tile')), may hold values from -6 to 6
- pair_patch: int32 [4096], P(('band', 'tile')), may hold values from 0 to 63
- pair_atm: int32 [4096], P(('band', 'tile')), may hold values from 0 to 4095, as said below
- numerators: int32 [4096, 128, 32], P(('band', 'tile')), may hold values from 0 to 16777215
- counts: int32 [32], P(('band', 'tile')), may hold values from 32 to 128, as said below
Outputs:
- atmosphere: float32 [131072, 128], P(('band', 'tile'))
Inputs may be any that keep to these rules, and one draw needn't show every extreme that they name: Block pair_atm[g] is owned by device pair_atm[g] // 128 (band-major device order). Every live pair of device (b, t) targets an owner in band b (any tile) or one of (b - 1, t), (b + 1, t). Among one device's live pairs at most 32 target one owner and at most 16 distinct blocks of one owner; both are reached on some device in every draw. Slots that are not live hold arbitrary blocks in range. `counts`: the value 128 occurs on some device in every draw.
All inputs are finite; a program needn't handle non-finite values.
Results may differ from a plain program's by a relative error of at most 0.0026.
Values sent between devices are 32-bit elements; how exact they have to be, the bound alone decides.
A program may use at most 64 MiB of HBM per device.

v0:
```python
import functools

import jax
import jax.numpy as jnp
from jax import lax
from jax.experimental import pallas as pl
from jax.experimental.pallas import tpu as pltpu
from jax.sharding import PartitionSpec as P

CELLS_DEV = 4096
SCALE = 2.0 ** (-27)
MESH = pl.DeviceIdType.MESH
LANES = 128
VMEM_LIMIT = 20 * 2 ** 20
STREAM_LIMIT = 24 * 2 ** 20
PADDED_LIMIT = 63 * 2 ** 20


def partners(count):
    if count & (count - 1) == 0:
        return [lambda me, k=k: me ^ k for k in range(count - 1, 0, -1)]
    return [lambda me, k=k: lax.rem(me + k, count) for k in range(1, count)]


def pack_kernel(tiles, bucket, blocks_owned, chunk,
                patch_ref, atm_ref, counts_ref, patches_hbm, numer_hbm,
                send_ref, labels_ref,
                patches_v, numer_v, table, used, patch_sem, numer_sems):
    pairs = numer_v.shape[0]
    patch_rows = numer_v.shape[2]
    chunks = pairs // chunk
    buckets = tiles + 2
    patch_copy = pltpu.make_async_copy(patches_hbm, patches_v, patch_sem)
    patch_copy.start()
    copies = []
    for c in range(chunks):
        part = pl.ds(c * chunk, chunk)
        copy = pltpu.make_async_copy(numer_hbm.at[part], numer_v.at[part], numer_sems.at[c])
        copy.start()
        copies.append(copy)
    band = lax.axis_index("band")
    live = counts_ref[0]

    for b in range(buckets):
        used[b] = 0

        @pl.loop(0, blocks_owned, unroll=16)
        def _(i):
            table[b * blocks_owned + i] = -1

        for s in range(bucket):
            labels_ref[b, 0, s] = -1
    patch_copy.wait()
    for c in range(chunks):
        copies[c].wait()

        @pl.when(c * chunk < live)
        def _():
            for j in range(chunk):
                g = c * chunk + j
                is_live = g < live
                atm = atm_ref[g]
                owner = lax.div(atm, blocks_owned)
                block = lax.rem(atm, blocks_owned)
                owner_band = lax.div(owner, tiles)
                owner_tile = lax.rem(owner, tiles)
                b = jnp.where(owner_band == band, owner_tile,
                              jnp.where(owner_band > band, tiles, tiles + 1))
                entry = b * blocks_owned + block
                known = table[entry]
                fresh = known < 0
                new = used[b]
                rank = jnp.where(fresh, new, known)

                @pl.when(is_live)
                def _():
                    table[entry] = rank
                    used[b] = jnp.where(fresh, new + 1, new)
                    labels_ref[b, 0, rank] = block

                slot = jnp.where(is_live, b * bucket + rank, buckets * bucket)
                rows = pl.multiple_of(patch_ref[g] * patch_rows, patch_rows)
                weight = (numer_v[g].astype(jnp.float32) * SCALE).astype(jnp.bfloat16)
                part = jnp.dot(weight, patches_v[pl.ds(rows, patch_rows), :],
                               preferred_element_type=jnp.float32)
                before = send_ref[slot]
                send_ref[slot] = jnp.where(fresh, part, before + part)


def send_kernel(tiles, bands, bucket, send_ref, labels_ref, recv_ref, recv_labels_ref,
                data_send, data_recv, label_send, label_recv):
    band, tile = lax.axis_index("band"), lax.axis_index("tile")
    barrier = pltpu.get_barrier_semaphore()
    steps = partners(tiles)
    for step in steps:
        pl.semaphore_signal(barrier, inc=1, device_id=(band, step(tile)), device_id_type=MESH)

    @pl.when(band < bands - 1)
    def _():
        pl.semaphore_signal(barrier, inc=1, device_id=(band + 1, tile), device_id_type=MESH)

    @pl.when(band > 0)
    def _():
        pl.semaphore_signal(barrier, inc=1, device_id=(band - 1, tile), device_id_type=MESH)

    neighbours = jnp.where(band < bands - 1, 1, 0) + jnp.where(band > 0, 1, 0)
    pl.semaphore_wait(barrier, tiles - 1 + neighbours)

    def pair(source, place, device, sem):
        rows = pl.ds(source * bucket, bucket)
        landing = pl.ds(place * bucket, bucket)
        return (
            pltpu.make_async_remote_copy(
                src_ref=labels_ref.at[source], dst_ref=recv_labels_ref.at[place],
                send_sem=label_send.at[sem], recv_sem=label_recv.at[sem],
                device_id=device, device_id_type=MESH),
            pltpu.make_async_remote_copy(
                src_ref=send_ref.at[rows], dst_ref=recv_ref.at[landing],
                send_sem=data_send.at[sem], recv_sem=data_recv.at[sem],
                device_id=device, device_id_type=MESH),
        )

    inside = [pair(step(tile), tile, (band, step(tile)), k) for k, step in enumerate(steps)]
    upward = pair(tiles, tiles, (band + 1, tile), tiles - 1)
    downward = pair(tiles + 1, tiles + 1, (band - 1, tile), tiles)
    for copies in inside[:2]:
        for copy in copies:
            copy.start()

    @pl.when(band < bands - 1)
    def _():
        for copy in upward:
            copy.start()

    @pl.when(band > 0)
    def _():
        for copy in downward:
            copy.start()

    for copies in inside[2:]:
        for copy in copies:
            copy.start()
    for copies in inside:
        for copy in copies:
            copy.wait()

    @pl.when(band < bands - 1)
    def _():
        for up, down in zip(upward, downward):
            up.wait_send()
            down.wait_recv()

    @pl.when(band > 0)
    def _():
        for up, down in zip(upward, downward):
            down.wait_send()
            up.wait_recv()


def add_kernel(tiles, bands, bucket, labels_ref, recv_labels_ref, send_hbm, recv_hbm, out_ref,
               landed, sems):
    band, tile = lax.axis_index("band"), lax.axis_index("tile")
    buckets = tiles + 2

    def copy_of(b, ref):
        rows = pl.ds(b * bucket, bucket)
        return pltpu.make_async_copy(ref.at[rows], landed.at[rows], sems.at[b])

    for b in range(buckets):
        if b < tiles:
            @pl.when(tile == b)
            def _():
                copy_of(b, send_hbm).start()

            @pl.when(tile != b)
            def _():
                copy_of(b, recv_hbm).start()
        else:
            copy_of(b, recv_hbm).start()
    out_ref[...] = jnp.zeros_like(out_ref)
    for b in range(buckets):
        copy_of(b, recv_hbm).wait()
        if b == tiles:
            valid = band > 0
        elif b == tiles + 1:
            valid = band < bands - 1
        else:
            valid = True
        for s in range(bucket):
            label = recv_labels_ref[b, 0, s]
            if b < tiles:
                label = jnp.where(tile == b, labels_ref[b, 0, s], label)

            @pl.when((label >= 0) & valid)
            def _():
                out_ref[label] += landed[b * bucket + s]


def per_device(tiles, bands, patches, pair_patch, pair_atm, numerators, counts):
    pairs, cell_rows, patch_rows = numerators.shape
    flux = patches.shape[1]
    blocks_owned = CELLS_DEV // cell_rows
    bucket = pairs // 8
    buckets = tiles + 2
    chunk = 16
    smem = pl.BlockSpec(memory_space=pltpu.SMEM)
    vmem = pl.BlockSpec(memory_space=pltpu.VMEM)
    anywhere = pl.BlockSpec(memory_space=pl.ANY)
    labels_shape = jax.ShapeDtypeStruct((buckets, 1, LANES), jnp.int32)
    recv_shape = jax.ShapeDtypeStruct((buckets * bucket, cell_rows, flux), jnp.float32)
    send, labels = pl.pallas_call(
        functools.partial(pack_kernel, tiles, bucket, blocks_owned, chunk),
        out_shape=(jax.ShapeDtypeStruct((buckets * bucket + 1, cell_rows, flux), jnp.float32), labels_shape),
        in_specs=[smem, smem, smem, anywhere, anywhere],
        out_specs=(vmem, smem),
        scratch_shapes=[
            pltpu.VMEM(patches.shape, patches.dtype),
            pltpu.VMEM((pairs, cell_rows, patch_rows), jnp.int32),
            pltpu.SMEM((buckets * blocks_owned,), jnp.int32),
            pltpu.SMEM((buckets,), jnp.int32),
            pltpu.SemaphoreType.DMA,
            pltpu.SemaphoreType.DMA((pairs // chunk,)),
        ],
        compiler_params=pltpu.CompilerParams(vmem_limit_bytes=PADDED_LIMIT),
        name="pack",
    )(pair_patch, pair_atm, counts, patches, numerators)
    recv, recv_labels = pl.pallas_call(
        functools.partial(send_kernel, tiles, bands, bucket),
        out_shape=(recv_shape, labels_shape),
        in_specs=[anywhere, anywhere],
        out_specs=(anywhere, anywhere),
        scratch_shapes=[pltpu.SemaphoreType.DMA((tiles + 1,))] * 4,
        compiler_params=pltpu.CompilerParams(collective_id=0, has_side_effects=True, vmem_limit_bytes=VMEM_LIMIT),
        name="exchange",
    )(send, labels)
    out = pl.pallas_call(
        functools.partial(add_kernel, tiles, bands, bucket),
        out_shape=jax.ShapeDtypeStruct((blocks_owned, cell_rows, flux), jnp.float32),
        in_specs=[smem, smem, anywhere, anywhere],
        out_specs=vmem,
        scratch_shapes=[
            pltpu.VMEM(recv_shape.shape, jnp.float32),
            pltpu.SemaphoreType.DMA((buckets,)),
        ],
        compiler_params=pltpu.CompilerParams(vmem_limit_bytes=VMEM_LIMIT),
        name="add",
    )(labels, recv_labels, send, recv)
    return out.reshape(blocks_owned * cell_rows, flux)


def ring_order(tiles):
    wide = tiles // 4
    if wide * 4 != tiles or wide % 2:
        return list(range(tiles))
    order = list(range(wide))
    for step, column in enumerate(reversed(range(wide))):
        rows = range(1, 4) if step % 2 == 0 else range(3, 0, -1)
        order += [row * wide + column for row in rows]
    return order


def chosen(values, index):
    picked = values[0]
    for k in range(1, len(values)):
        picked = jnp.where(index == k, values[k], picked)
    return picked


def ring_tile(tiles, tile, steps):
    order = ring_order(tiles)
    position = chosen([order.index(k) for k in range(tiles)], tile)
    return chosen(order, lax.rem(position + steps + tiles, tiles))


def layout(bucket):
    return dict(up=4 * bucket, down=5 * bucket, own=6 * bucket, end=7 * bucket)


def reaching(tiles, bucket, way, read):
    reach = tiles // 2
    base = 7 * bucket - 1
    far = read(base + reach)
    counts = [read(base + (k if way == 0 else tiles - k)) for k in range(1, reach)]
    counts.append((far + 1) >> 1 if way == 0 else far >> 1)
    beyond = [0]
    for count in reversed(counts):
        beyond.append(beyond[-1] + count)
    return [None] + beyond[::-1]


def split(value, size):
    if size & (size - 1) == 0:
        return value >> (size.bit_length() - 1), value & (size - 1)
    return lax.div(value, size), lax.rem(value, size)


def sort_pairs(tiles, bands, bucket, blocks_owned, band, tile, live, atm):
    pairs = atm.shape[1]
    reach = tiles // 2
    order = ring_order(tiles)
    spots = [order.index(k) for k in range(tiles)]
    here = chosen(spots, tile)
    wide = (pairs, pairs)

    def across(value):
        return jnp.broadcast_to(value, wide).T

    def least(value):
        return jnp.min(value, axis=0, keepdims=True)

    def most(value):
        return jnp.max(value, axis=0, keepdims=True)

    def count(mask):
        return jnp.sum(jnp.where(mask, 1, 0), axis=0, keepdims=True)

    def bucket_of(value):
        owner, block = split(value, blocks_owned)
        owner_band, owner_tile = split(owner, tiles)
        ahead = split(chosen(spots, owner_tile) - here + tiles, tiles)[1]
        return jnp.where(owner_band == band, ahead, jnp.where(owner_band > band, tiles, tiles + 1)), block

    row = lax.broadcasted_iota(jnp.int32, wide, 0)
    lane = lax.broadcasted_iota(jnp.int32, wide, 1)
    one_lane = lax.broadcasted_iota(jnp.int32, (1, pairs), 1)
    atm_c = across(atm)
    live_c = row < live
    same = (atm_c == atm) & live_c
    first = least(jnp.where(same, row, pairs))
    before = most(jnp.where(same & (row < lane), row, -1))
    fresh_c = (across(first) == row) & live_c
    b, _ = bucket_of(atm)
    b_c, block_c = bucket_of(atm_c)
    rank = count(fresh_c & (b_c == b) & (row < first))
    back = (b > reach) | ((b == reach) & ((rank & 1) == 1))
    region = jnp.where(b == 0, 4, jnp.where(b >= tiles, b - tiles + 2, jnp.where(back, 1, 0)))
    near = jnp.where(region == 0, reach - b, jnp.where(region == 1, b - reach, 0))
    shift = ((reach + 1) * (pairs + 1)).bit_length()
    key = (region << shift) + near * (pairs + 1) + first
    key_c = across(key)
    place = count(fresh_c & ((key_c >> shift) == region) & (key_c < key))
    ring = region < 2
    room = jnp.where(ring, 2 * bucket, bucket)
    base = jnp.where(ring, 2 * region, region + 2) * bucket
    fits = place < room
    slot = jnp.where((one_lane < live) & fits, base + place, pairs)
    overflow = jnp.max(jnp.where((one_lane < live) & jnp.logical_not(fits), 1, 0), axis=1, keepdims=True)
    hit = across(slot) == lane
    last = most(jnp.where(hit, row, 0))
    label = most(jnp.where(hit, block_c, -1))
    counts = count(fresh_c & (b_c == lane - (7 * bucket - 1)))
    labels = jnp.where(one_lane < 7 * bucket, label, jnp.where(one_lane == pairs - 1, overflow, counts))
    return before, last, labels


def starts(reach, lag, reaches):
    first = [None] * (reach + 1)
    for u in range(reach - 1, -1, -1):
        begin = [0]
        for j in range(1, reach - u):
            after = begin[j - 1] + reaches[u + j - 1][j]
            begin.append(jnp.maximum(after, first[u + 1][j - 1] + lag))
        first[u] = begin
    end = first[0][reach - 1] + reaches[reach - 1][reach]
    return first[0], first[1], end


def stream_kernel(tiles, bands, bucket, blocks_owned, plans, group,
                  patch_ref, counts_ref, atm_ref, patches_hbm, numer_hbm,
                  pool_ref, beside_ref, own_ref, table_ref, plan_ref,
                  patches_ref, numer_ref, labels_ref, work_v, work_ref, load_sems, sums, side, stage, recv, landing, marks, mark,
                  ring_send, ring_recv, beside_send, beside_recv, label_send, label_recv, local_sem):
    band, tile = lax.axis_index("band"), lax.axis_index("tile")
    reach = tiles // 2
    own_rows = 2 * bucket
    at = layout(bucket)
    steps = partners(tiles)
    pairs = numer_ref.shape[0]

    def numer_load(c):
        part = pl.ds(c * group, group)
        return pltpu.make_async_copy(numer_hbm.at[part], numer_ref.at[part], load_sems.at[c])

    patch_load = pltpu.make_async_copy(patches_hbm, patches_ref, load_sems.at[pairs // group])
    patch_load.start()
    for c in range(pairs // group):
        numer_load(c).start()
    barrier = pltpu.get_barrier_semaphore()
    for step in steps:
        pl.semaphore_signal(barrier, inc=1, device_id=(band, step(tile)), device_id_type=MESH)
    for j in range(1, bands):
        pl.semaphore_signal(barrier, inc=1, device_id=(lax.rem(band + j, bands), tile), device_id_type=MESH)
    before, last, labels = sort_pairs(tiles, bands, bucket, blocks_owned, band, tile, counts_ref[0], atm_ref[...])
    labels_ref[...] = labels
    landing[tile] = labels
    work_v[0:1] = before
    work_v[1:2] = last
    work_in = pltpu.make_async_copy(work_v, work_ref, local_sem)
    work_in.start()
    work_in.wait()
    patch_load.wait()

    @pl.loop(0, pairs // group)
    def _(c):
        numer_load(c).wait()
        for j in range(group):
            g = c * group + j
            weight = (numer_ref[g].astype(jnp.float32) * SCALE).astype(jnp.bfloat16)
            part = jnp.dot(weight, patches_ref[patch_ref[g]], preferred_element_type=jnp.float32)
            before = work_ref[0, g]
            earlier = sums[jnp.maximum(before, 0)]
            sums[g] = part + jnp.where(before >= 0, earlier, 0.0)

    def total(slot):
        return sums[work_ref[1, slot]]

    targets = ((band, ring_tile(tiles, tile, 1)), (band, ring_tile(tiles, tile, -1)))
    is_edge = (band == 0) | (band == bands - 1)
    head = max(size * lag for size, _, lag in plans)
    for way in range(2):
        for s in range(head):
            pool_ref[way, s] = total(way * own_rows + s)
    pl.semaphore_wait(barrier, tiles + bands - 2)
    inside = [
        pltpu.make_async_remote_copy(
            src_ref=labels_ref, dst_ref=landing.at[tile],
            send_sem=label_send.at[k], recv_sem=label_recv.at[k],
            device_id=(band, step(tile)), device_id_type=MESH)
        for k, step in enumerate(steps)
    ]
    across = [
        pltpu.make_async_remote_copy(
            src_ref=mark, dst_ref=marks.at[band],
            send_sem=label_send.at[tiles - 2 + j], recv_sem=label_recv.at[tiles - 2 + j],
            device_id=(lax.rem(band + j, bands), tile), device_id_type=MESH)
        for j in range(1, bands)
    ]
    for copy in inside:
        copy.start()

    def hop(way, r, size, source):
        rows = pl.ds(r * size, size)
        return pltpu.make_async_remote_copy(
            src_ref=source, dst_ref=recv.at[way, rows],
            send_sem=ring_send.at[way, r], recv_sem=ring_recv.at[way, r],
            device_id=targets[way], device_id_type=MESH)

    def own_hop(way, r, size):
        return hop(way, r, size, pool_ref.at[way, pl.ds(r * size, size)])

    def later_hop(way, r, size):
        return hop(way, r, size, stage.at[way, pl.ds(r * size, size)])

    for edge in (True, False):
        size, rounds, lag = plans[0 if edge else 1]

        @pl.when(is_edge if edge else jnp.logical_not(is_edge))
        def _():
            for r in range(lag):
                for way in range(2):
                    own_hop(way, r, size).start()

    def beside(way, target_band):
        return pltpu.make_async_remote_copy(
            src_ref=side.at[way], dst_ref=beside_ref.at[way],
            send_sem=beside_send.at[way], recv_sem=beside_recv.at[way],
            device_id=(target_band, tile), device_id_type=MESH)

    upward, downward = beside(0, band + 1), beside(1, band - 1)
    for way in range(2):
        for s in range(bucket):
            side[way, s] = total(at["up"] + way * bucket + s)
    for way in range(2):
        for s in range(head, own_rows):
            pool_ref[way, s] = total(way * own_rows + s)
    for s in range(bucket):
        own_ref[s] = total(at["own"] + s)

    @pl.when(band < bands - 1)
    def _():
        upward.start()

    @pl.when(band > 0)
    def _():
        downward.start()

    for copy in inside:
        copy.wait()
    rows_in = pltpu.make_async_copy(landing, table_ref.at[pl.ds(0, tiles)], local_sem)
    rows_in.start()
    rows_in.wait()

    upstream = [[ring_tile(tiles, tile, -u if way == 0 else u) for u in range(tiles)] for way in range(2)]
    reaches = [[reaching(tiles, bucket, way, lambda i, t=t: table_ref[t, 0, i]) for t in upstream[way]]
               for way in range(2)]
    lag_slots = jnp.where(is_edge, plans[0][0] * plans[0][2], plans[1][0] * plans[1][2])
    capacity = jnp.where(is_edge, plans[0][0] * plans[0][1], plans[1][0] * plans[1][1])
    worst = jnp.int32(0)
    flag = jnp.int32(0)
    begins = []
    for way in range(2):
        for v in range(tiles):
            ahead, behind, end = starts(reach, lag_slots, [reaches[way][(v + u) % tiles] for u in range(reach)])
            worst = jnp.maximum(worst, end)
            if v == 0:
                begins.append(ahead)
    arrivals = []
    for way in range(2):
        ahead, _, _ = starts(reach, lag_slots, [reaches[way][(1 + u) % tiles] for u in range(reach)])
        arrivals.append(ahead)
    for t in range(tiles):
        flag = jnp.maximum(flag, table_ref[t, 0, LANES - 1])
    flag = jnp.where(worst > capacity, 1, flag)
    lane = lax.broadcasted_iota(jnp.int32, (1, LANES), 1)
    mark[...] = jnp.where(lane == LANES - 1, flag, landing[tile])
    for way in range(2):
        for j in range(reach):
            plan_ref[0, 1 + way * reach + j] = arrivals[way][j]

    for edge in (True, False):
        size, rounds, lag = plans[0 if edge else 1]
        last_row = own_rows + size * rounds - 1

        @pl.when(is_edge if edge else jnp.logical_not(is_edge))
        def _():
            def keep(way, r):
                later_hop(way, r, size).wait_recv()
                pool_ref[way, pl.ds(own_rows + r * size, size)] = recv[way, pl.ds(r * size, size)]

            def gather(way, r):
                begin, arrived = begins[way], arrivals[way]
                for s in range(size):
                    p = r * size + s
                    row = jnp.minimum(p, own_rows - 1)
                    for j in range(1, reach):
                        row = jnp.where(p >= begin[j], p + (own_rows + arrived[j - 1] - begin[j]), row)
                    row = jnp.clip(row, 0, last_row)
                    stage[way, p] = pool_ref[way, row]

            def one_round(r):
                for way in range(2):
                    keep(way, r - lag)
                for way in range(2):
                    gather(way, r)
                for way in range(2):
                    later_hop(way, r, size).start()

            one_round(lag)
            for copy in across:
                copy.start()

            @pl.loop(lag + 1, rounds)
            def _(r):
                one_round(r)

            @pl.loop(rounds - lag, rounds)
            def _(r):
                for way in range(2):
                    keep(way, r)

            @pl.loop(0, rounds)
            def _(r):
                for way in range(2):
                    later_hop(way, r, size).wait_send()

    for copy in across:
        copy.wait()
    rows_over = pltpu.make_async_copy(marks, table_ref.at[pl.ds(tiles, bands)], local_sem)
    rows_over.start()
    rows_over.wait()
    for j in range(1, bands):
        flag = jnp.maximum(flag, table_ref[tiles + lax.rem(band + j, bands), 0, LANES - 1])
    plan_ref[0, 0] = flag

    @pl.when(band < bands - 1)
    def _():
        upward.wait_send()
        downward.wait_recv()

    @pl.when(band > 0)
    def _():
        downward.wait_send()
        upward.wait_recv()


def take_kernel(tiles, bands, bucket, table_ref, plan_ref, own_ref, pool_ref, beside_ref, out_ref):
    band, tile = lax.axis_index("band"), lax.axis_index("tile")
    reach = tiles // 2
    own_rows = 2 * bucket
    at = layout(bucket)
    out_ref[...] = jnp.zeros_like(out_ref)
    for s in range(bucket):
        label = table_ref[tile, 0, at["own"] + s]

        @pl.when(label >= 0)
        def _():
            out_ref[label] += own_ref[s]

    for way in range(2):
        other = tiles + jnp.clip(band - 1 if way == 0 else band + 1, 0, bands - 1)
        valid = (band > 0) if way == 0 else (band < bands - 1)
        for s in range(bucket):
            label = table_ref[other, 0, at["up"] + way * bucket + s]

            @pl.when((label >= 0) & valid)
            def _():
                out_ref[label] += beside_ref[way, s]

    for way in range(2):
        for distance in range(1, reach + 1):
            source = ring_tile(tiles, tile, -distance if way == 0 else distance)
            reaches = reaching(tiles, bucket, way, lambda i: table_ref[source, 0, i])
            start = own_rows + plan_ref[0, 1 + way * reach + distance - 1]

            @pl.loop(reaches[distance + 1], reaches[distance])
            def _(i):
                out_ref[table_ref[source, 0, way * own_rows + i]] += pool_ref[way, start + i]


def adaptive(tiles, bands, patches, pair_patch, pair_atm, numerators, counts):
    pairs, patch_rows, cell_rows = numerators.shape
    flux = patches.shape[1]
    blocks_owned = CELLS_DEV // cell_rows
    bucket = pairs // 8
    reach = tiles // 2
    group = 16
    plans = ((3, pl.cdiv(20 * reach, 3), 5), (2, 6 * reach, 5))
    slots = max(size * rounds for size, rounds, _ in plans)
    most = max(rounds for _, rounds, _ in plans)
    smem = pl.BlockSpec(memory_space=pltpu.SMEM)
    vmem = pl.BlockSpec(memory_space=pltpu.VMEM)
    hbm = pl.BlockSpec(memory_space=pltpu.HBM)
    block = (cell_rows, flux)
    f32 = jnp.float32
    numerators = jnp.transpose(numerators, (0, 2, 1))
    pool, beside, own, table, plan = pl.pallas_call(
        functools.partial(stream_kernel, tiles, bands, bucket, blocks_owned, plans, group),
        out_shape=(jax.ShapeDtypeStruct((2, 2 * bucket + slots) + block, f32),
                   jax.ShapeDtypeStruct((2, bucket) + block, f32),
                   jax.ShapeDtypeStruct((bucket,) + block, f32),
                   jax.ShapeDtypeStruct((tiles + bands, 1, LANES), jnp.int32),
                   jax.ShapeDtypeStruct((1, LANES), jnp.int32)),
        in_specs=[smem, smem, vmem, hbm, hbm],
        out_specs=(vmem, vmem, vmem, smem, smem),
        scratch_shapes=[
            pltpu.VMEM((patches.shape[0] // patch_rows, patch_rows, flux), patches.dtype),
            pltpu.VMEM(numerators.shape, numerators.dtype),
            pltpu.VMEM((1, LANES), jnp.int32),
            pltpu.VMEM((2, pairs), jnp.int32),
            pltpu.SMEM((2, pairs), jnp.int32),
            pltpu.SemaphoreType.DMA((pairs // group + 1,)),
            pltpu.VMEM((pairs,) + block, f32),
            pltpu.VMEM((2, bucket) + block, f32),
            pltpu.VMEM((2, slots) + block, f32),
            pltpu.VMEM((2, slots) + block, f32),
            pltpu.VMEM((tiles, 1, LANES), jnp.int32),
            pltpu.VMEM((bands, 1, LANES), jnp.int32),
            pltpu.VMEM((1, LANES), jnp.int32),
            pltpu.SemaphoreType.DMA((2, most)),
            pltpu.SemaphoreType.DMA((2, most)),
            pltpu.SemaphoreType.DMA((2,)),
            pltpu.SemaphoreType.DMA((2,)),
            pltpu.SemaphoreType.DMA((tiles + bands - 2,)),
            pltpu.SemaphoreType.DMA((tiles + bands - 2,)),
            pltpu.SemaphoreType.DMA,
        ],
        compiler_params=pltpu.CompilerParams(collective_id=1, has_side_effects=True, vmem_limit_bytes=STREAM_LIMIT),
        name="stream",
    )(pair_patch, counts, pair_atm.reshape(1, pairs), patches.reshape(-1, patch_rows, flux), numerators)

    def take(patches, pair_patch, pair_atm, numerators, counts, table, plan, own, pool, beside):
        out = pl.pallas_call(
            functools.partial(take_kernel, tiles, bands, bucket),
            out_shape=jax.ShapeDtypeStruct((blocks_owned,) + block, f32),
            in_specs=[smem, smem, vmem, vmem, vmem],
            out_specs=vmem,
            compiler_params=pltpu.CompilerParams(vmem_limit_bytes=VMEM_LIMIT),
            name="take",
        )(table, plan, own, pool, beside)
        return out.reshape(blocks_owned * cell_rows, flux)

    def padded(patches, pair_patch, pair_atm, numerators, counts, table, plan, own, pool, beside):
        return per_device(tiles, bands, patches, pair_patch, pair_atm, numerators, counts)

    return lax.cond(plan[0, 0] > 0, padded, take, patches, pair_patch, pair_atm, numerators, counts,
                    table, plan, own, pool, beside)


def solution(mesh):
    spec = P(("band", "tile"))
    placed = (
        P(("band", "tile"), None),
        spec,
        spec,
        P(("band", "tile"), None, None),
        spec,
    )
    body = functools.partial(adaptive, mesh.shape["tile"], mesh.shape["band"])
    return jax.shard_map(body, mesh=mesh, in_specs=placed, out_specs=P(("band", "tile"), None), check_vma=False)
```

profile of v0, /device:TPU:0, one launch (start us, length us, event | category | flops | bytes accessed | tf_op | source)
XLA Modules:
  0.0 39.2 jit_solution(9198431552253380294)
XLA Ops:
  0.7 0.0 copy-start.2
  0.7 0.0 copy-start.3
  0.7 35.8 %stream.1 = (f32[2,113,32,128]{3,2,1,0:T(8,128)S(1)}, f32[2,16,32,128]{3,2,1,0:T(8,128)S(1)}, f32[16,32,128]{2,1,0:T(8,128)S(1)}, s32[12,1,128]{2,1,0:T(1,128)S(1)}, s32[1,128]{1,0:T(1,128)S(1)}) custom-call(s32[128]{0:T(128)} %patch_ref.1, s32[1]{0:T(128)S(6)} %copy.10.counts_ref, s32[1,128]{1,0:T(1,128)} %bitcast.10, bf16[64,128,128]{2,1,0:T(8,128)(2,1)} %bitcast.7, ...), custom_call_target="tpu_custom_call" | custom-call | tf_op jit(solution)/shard_map/stream/pallas_call | solution.py:636
  36.5 0.0 copy-done.2
  36.5 0.0 copy-done.3
  36.5 2.7 %conditional.1 = (f32[4096,128]{1,0:T(8,128)}) conditional(s32[]{:T(128)} %bitcast.5, (s32[12,1,128]{2,1,0:T(1,128)S(1)}, s32[1,128]{1,0:T(1,128)S(1)}, f32[16,32,128]{2,1,0:T(8,128)S(1)}, f32[2,113,32,128]{3,2,1,0:T(8,128)S(1)}, f32[2,16,32,128]{3,2,1,0:T(8,128)S(1)}) %tuple.11, (s32[128]{0:T(128)S(1)}, s32[128]{0:T(128)S(1)}, s32[1]{0:T(128)}, ...), branch_computations={%region_0.0_spmd, %region_1.0_spmd} | conditional | bytes 10571840 | solution.py:685
  36.5 2.7 %take.1 = f32[128,32,128]{2,1,0:T(8,128)} custom-call(s32[12,1,128]{2,1,0:T(1,128)S(1)} %get-tuple-element.28.table_ref, s32[1,128]{1,0:T(1,128)S(1)} %get-tuple-element.29.plan_ref, f32[16,32,128]{2,1,0:T(8,128)S(1)} %get-tuple-element.30.own_ref, f32[2,113,32,128]{3,2,1,0:T(8,128)S(1)} %get-tuple-element.31.pool_ref, ...), custom_call_target="tpu_custom_call" | custom-call | tf_op jit(solution)/shard_map/cond/branch_0_fun/take/pallas_call | solution.py:672
Async XLA Ops:
  0.7 35.8 %copy-start.2 = (s32[128]{0:T(128)S(1)}, s32[128]{0:T(128)}, u32[]{:S(2)}) copy-start(s32[128]{0:T(128)} %patch_ref.1) | copy-start | bytes 1540
  0.7 35.8 %copy-start.3 = (s32[128]{0:T(128)S(1)}, s32[128]{0:T(128)}, u32[]{:S(2)}) copy-start(s32[128]{0:T(128)} %param.9) | copy-start | bytes 1540
where the time goes:
time: 39.5 us; the launch traced here: 39.2 us
  Pallas kernels  38.4 us (97%)
  between operations  0.73 us (2%)
    pallas_call x1, Pallas kernels, adaptive(): pl.pallas_call(functools.partial(stream_kernel, tiles, bands, bucket, blo...  35.8 us
    pallas_call x1, Pallas kernels, take(): pl.pallas_call(functools.partial(take_kernel, tiles, bands, bucket), out_...  2.69 us

commit v1 on v0

--- a/solution.py
+++ b/solution.py
@@ -349,7 +349,9 @@
     last = most(jnp.where(hit, row, 0))
     label = most(jnp.where(hit, block_c, -1))
     counts = count(fresh_c & (b_c == lane - (7 * bucket - 1)))
-    labels = jnp.where(one_lane < 7 * bucket, label, jnp.where(one_lane == pairs - 1, overflow, counts))
+    kinds = [count(fresh_c & (b_c == k)) for k in (0, tiles, tiles + 1)]
+    packed = overflow + sum(kind << (1 + 6 * i) for i, kind in enumerate(kinds))
+    labels = jnp.where(one_lane < 7 * bucket, label, jnp.where(one_lane == pairs - 1, packed, counts))
     return before, last, labels
 
 
@@ -361,7 +363,10 @@
             after = begin[j - 1] + reaches[u + j - 1][j]
             begin.append(jnp.maximum(after, first[u + 1][j - 1] + lag))
         first[u] = begin
-    end = first[0][reach - 1] + reaches[reach - 1][reach]
+    end = jnp.int32(0)
+    for j in range(reach):
+        size = reaches[j][j + 1]
+        end = jnp.where(size > 0, first[0][j] + size, end)
     return first[0], first[1], end
 
 
@@ -509,10 +514,11 @@
         ahead, _, _ = starts(reach, lag_slots, [reaches[way][(1 + u) % tiles] for u in range(reach)])
         arrivals.append(ahead)
     for t in range(tiles):
-        flag = jnp.maximum(flag, table_ref[t, 0, LANES - 1])
+        flag = jnp.maximum(flag, table_ref[t, 0, LANES - 1] & 1)
     flag = jnp.where(worst > capacity, 1, flag)
     lane = lax.broadcasted_iota(jnp.int32, (1, LANES), 1)
-    mark[...] = jnp.where(lane == LANES - 1, flag, landing[tile])
+    row = landing[tile]
+    mark[...] = jnp.where(lane == LANES - 1, row - (row & 1) + flag, row)
     for way in range(2):
         for j in range(reach):
             plan_ref[0, 1 + way * reach + j] = arrivals[way][j]
@@ -540,9 +546,7 @@
             def one_round(r):
                 for way in range(2):
                     keep(way, r - lag)
-                for way in range(2):
                     gather(way, r)
-                for way in range(2):
                     later_hop(way, r, size).start()
 
             one_round(lag)
@@ -569,7 +573,7 @@
     rows_over.start()
     rows_over.wait()
     for j in range(1, bands):
-        flag = jnp.maximum(flag, table_ref[tiles + lax.rem(band + j, bands), 0, LANES - 1])
+        flag = jnp.maximum(flag, table_ref[tiles + lax.rem(band + j, bands), 0, LANES - 1] & 1)
     plan_ref[0, 0] = flag
 
     @pl.when(band < bands - 1)
@@ -589,22 +593,21 @@
     own_rows = 2 * bucket
     at = layout(bucket)
     out_ref[...] = jnp.zeros_like(out_ref)
-    for s in range(bucket):
-        label = table_ref[tile, 0, at["own"] + s]
-
-        @pl.when(label >= 0)
-        def _():
-            out_ref[label] += own_ref[s]
+
+    def how_many(row, kind):
+        return (table_ref[row, 0, LANES - 1] >> (1 + 6 * kind)) & 63
+
+    @pl.loop(0, how_many(tile, 0))
+    def _(i):
+        out_ref[table_ref[tile, 0, at["own"] + i]] += own_ref[i]
 
     for way in range(2):
         other = tiles + jnp.clip(band - 1 if way == 0 else band + 1, 0, bands - 1)
         valid = (band > 0) if way == 0 else (band < bands - 1)
-        for s in range(bucket):
-            label = table_ref[other, 0, at["up"] + way * bucket + s]
-
-            @pl.when((label >= 0) & valid)
-            def _():
-                out_ref[label] += beside_ref[way, s]
+
+        @pl.loop(0, jnp.where(valid, how_many(other, 1 + way), 0))
+        def _(i):
+            out_ref[table_ref[other, 0, at["up"] + way * bucket + i]] += beside_ref[way, i]
 
     for way in range(2):
         for distance in range(1, reach + 1):
@@ -624,7 +627,7 @@
     bucket = pairs // 8
     reach = tiles // 2
     group = 16
-    plans = ((3, pl.cdiv(20 * reach, 3), 5), (2, 6 * reach, 5))
+    plans = ((5, 4 * reach, 4), (3, 4 * reach, 3))
     slots = max(size * rounds for size, rounds, _ in plans)
     most = max(rounds for _, rounds, _ in plans)
     smem = pl.BlockSpec(memory_space=pltpu.SMEM)

time: 39.5 us -> 37.2 us (0.942)
  Pallas kernels: 38.4 us -> 36.4 us
    pallas_call x1, Pallas kernels: 35.8 us -> 33.6 us  [adaptive(): pl.pallas_call(functools.partial(stream_kernel, tiles, bands, bucket, blo...]
where the time goes in v1:
time: 37.2 us
  Pallas kernels  36.4 us (98%)
  between operations  0.73 us (2%)
    pallas_call x1, Pallas kernels, adaptive(): pl.pallas_call(functools.partial(stream_kernel, tiles, bands, bucket, blo...  33.6 us
    pallas_call x1, Pallas kernels, take(): pl.pallas_call(functools.partial(take_kernel, tiles, bands, bucket), out_...  2.85 us

profile of v1, /device:TPU:0, one launch (start us, length us, event | category | flops | bytes accessed | tf_op | source)
XLA Modules:
  0.0 37.2 jit_solution(8569594878862323838)
XLA Ops:
  0.7 0.0 copy-start.2
  0.7 0.0 copy-start.3
  0.7 33.6 %stream.1 = (f32[2,112,32,128]{3,2,1,0:T(8,128)S(1)}, f32[2,16,32,128]{3,2,1,0:T(8,128)S(1)}, f32[16,32,128]{2,1,0:T(8,128)S(1)}, s32[12,1,128]{2,1,0:T(1,128)S(1)}, s32[1,128]{1,0:T(1,128)S(1)}) custom-call(s32[128]{0:T(128)} %patch_ref.1, s32[1]{0:T(128)S(6)} %copy.10.counts_ref, s32[1,128]{1,0:T(1,128)} %bitcast.10, bf16[64,128,128]{2,1,0:T(8,128)(2,1)} %bitcast.7, ...), custom_call_target="tpu_custom_call" | custom-call | tf_op jit(solution)/shard_map/stream/pallas_call | solution.py:639
  34.3 0.0 copy-done.2
  34.3 0.0 copy-done.3
  34.3 2.9 %conditional.1 = (f32[4096,128]{1,0:T(8,128)}) conditional(s32[]{:T(128)} %bitcast.5, (s32[12,1,128]{2,1,0:T(1,128)S(1)}, s32[1,128]{1,0:T(1,128)S(1)}, f32[16,32,128]{2,1,0:T(8,128)S(1)}, f32[2,112,32,128]{3,2,1,0:T(8,128)S(1)}, f32[2,16,32,128]{3,2,1,0:T(8,128)S(1)}) %tuple.11, (s32[128]{0:T(128)S(1)}, s32[128]{0:T(128)S(1)}, s32[1]{0:T(128)}, ...), branch_computations={%region_0.0_spmd, %region_1.0_spmd} | conditional | bytes 10571840 | solution.py:688
  34.3 2.9 %take.1 = f32[128,32,128]{2,1,0:T(8,128)} custom-call(s32[12,1,128]{2,1,0:T(1,128)S(1)} %get-tuple-element.28.table_ref, s32[1,128]{1,0:T(1,128)S(1)} %get-tuple-element.29.plan_ref, f32[16,32,128]{2,1,0:T(8,128)S(1)} %get-tuple-element.30.own_ref, f32[2,112,32,128]{3,2,1,0:T(8,128)S(1)} %get-tuple-element.31.pool_ref, ...), custom_call_target="tpu_custom_call" | custom-call | tf_op jit(solution)/shard_map/cond/branch_0_fun/take/pallas_call | solution.py:675
Async XLA Ops:
  0.7 33.6 %copy-start.2 = (s32[128]{0:T(128)S(1)}, s32[128]{0:T(128)}, u32[]{:S(2)}) copy-start(s32[128]{0:T(128)} %patch_ref.1) | copy-start | bytes 1540
  0.7 33.6 %copy-start.3 = (s32[128]{0:T(128)S(1)}, s32[128]{0:T(128)}, u32[]{:S(2)}) copy-start(s32[128]{0:T(128)} %param.9) | copy-start | bytes 1540

commit v2 on v1

--- a/solution.py
+++ b/solution.py
@@ -372,8 +372,8 @@
 
 def stream_kernel(tiles, bands, bucket, blocks_owned, plans, group,
                   patch_ref, counts_ref, atm_ref, patches_hbm, numer_hbm,
-                  pool_ref, beside_ref, own_ref, table_ref, plan_ref,
-                  patches_ref, numer_ref, labels_ref, work_v, work_ref, load_sems, sums, side, stage, recv, landing, marks, mark,
+                  pool_ref, beside_ref, own_ref, landing, flag_ref,
+                  patches_ref, numer_ref, labels_ref, work_v, work_ref, load_sems, sums, side, stage, recv, table_ref, mark,
                   ring_send, ring_recv, beside_send, beside_recv, label_send, label_recv, local_sem):
     band, tile = lax.axis_index("band"), lax.axis_index("tile")
     reach = tiles // 2
@@ -435,7 +435,7 @@
     ]
     across = [
         pltpu.make_async_remote_copy(
-            src_ref=mark, dst_ref=marks.at[band],
+            src_ref=mark, dst_ref=landing.at[tiles + band],
             send_sem=label_send.at[tiles - 2 + j], recv_sem=label_recv.at[tiles - 2 + j],
             device_id=(lax.rem(band + j, bands), tile), device_id_type=MESH)
         for j in range(1, bands)
@@ -491,7 +491,7 @@
 
     for copy in inside:
         copy.wait()
-    rows_in = pltpu.make_async_copy(landing, table_ref.at[pl.ds(0, tiles)], local_sem)
+    rows_in = pltpu.make_async_copy(landing.at[pl.ds(0, tiles)], table_ref.at[pl.ds(0, tiles)], local_sem)
     rows_in.start()
     rows_in.wait()
 
@@ -519,9 +519,11 @@
     lane = lax.broadcasted_iota(jnp.int32, (1, LANES), 1)
     row = landing[tile]
     mark[...] = jnp.where(lane == LANES - 1, row - (row & 1) + flag, row)
+    plan = jnp.zeros((1, LANES), jnp.int32)
     for way in range(2):
         for j in range(reach):
-            plan_ref[0, 1 + way * reach + j] = arrivals[way][j]
+            plan = jnp.where(lane == way * reach + j, arrivals[way][j], plan)
+    landing[tiles + bands] = plan
 
     for edge in (True, False):
         size, rounds, lag = plans[0 if edge else 1]
@@ -557,24 +559,14 @@
             def _(r):
                 one_round(r)
 
-            @pl.loop(rounds - lag, rounds)
-            def _(r):
-                for way in range(2):
-                    keep(way, r)
-
-            @pl.loop(0, rounds)
-            def _(r):
-                for way in range(2):
-                    later_hop(way, r, size).wait_send()
-
     for copy in across:
         copy.wait()
-    rows_over = pltpu.make_async_copy(marks, table_ref.at[pl.ds(tiles, bands)], local_sem)
+    rows_over = pltpu.make_async_copy(landing.at[pl.ds(tiles, bands)], table_ref.at[pl.ds(tiles, bands)], local_sem)
     rows_over.start()
     rows_over.wait()
     for j in range(1, bands):
         flag = jnp.maximum(flag, table_ref[tiles + lax.rem(band + j, bands), 0, LANES - 1] & 1)
-    plan_ref[0, 0] = flag
+    flag_ref[0] = flag
 
     @pl.when(band < bands - 1)
     def _():
@@ -586,38 +578,63 @@
         downward.wait_send()
         upward.wait_recv()
 
-
-def take_kernel(tiles, bands, bucket, table_ref, plan_ref, own_ref, pool_ref, beside_ref, out_ref):
+    for edge in (True, False):
+        size, rounds, lag = plans[0 if edge else 1]
+
+        @pl.when(is_edge if edge else jnp.logical_not(is_edge))
+        def _():
+            @pl.loop(0, rounds - lag)
+            def _(r):
+                for way in range(2):
+                    later_hop(way, r, size).wait_send()
+
+            @pl.loop(rounds - lag, rounds)
+            def _(r):
+                for way in range(2):
+                    later_hop(way, r, size).wait()
+                    pool_ref[way, pl.ds(own_rows + r * size, size)] = recv[way, pl.ds(r * size, size)]
+
+
+def take_kernel(tiles, bands, bucket, table_ref, own_ref, pool_ref, beside_ref, out_ref):
     band, tile = lax.axis_index("band"), lax.axis_index("tile")
     reach = tiles // 2
     own_rows = 2 * bucket
     at = layout(bucket)
     out_ref[...] = jnp.zeros_like(out_ref)
 
-    def how_many(row, kind):
-        return (table_ref[row, 0, LANES - 1] >> (1 + 6 * kind)) & 63
-
-    @pl.loop(0, how_many(tile, 0))
-    def _(i):
-        out_ref[table_ref[tile, 0, at["own"] + i]] += own_ref[i]
-
+    def how_many(lane, kind):
+        return (lane >> (1 + 6 * kind)) & 63
+
+    def add(low, high, label_of, block_of):
+        fours = (high - low) >> 2
+
+        @pl.loop(0, fours)
+        def _(k):
+            at_once = [low + 4 * k + j for j in range(4)]
+            labels = [label_of(i) for i in at_once]
+            sums = [out_ref[label] + block_of(i) for label, i in zip(labels, at_once)]
+            for label, total in zip(labels, sums):
+                out_ref[label] = total
+
+        @pl.loop(low + 4 * fours, high)
+        def _(i):
+            out_ref[label_of(i)] += block_of(i)
+
+    add(0, how_many(table_ref[tile, 0, LANES - 1], 0),
+        lambda i: table_ref[tile, 0, at["own"] + i], lambda i: own_ref[i])
     for way in range(2):
         other = tiles + jnp.clip(band - 1 if way == 0 else band + 1, 0, bands - 1)
         valid = (band > 0) if way == 0 else (band < bands - 1)
-
-        @pl.loop(0, jnp.where(valid, how_many(other, 1 + way), 0))
-        def _(i):
-            out_ref[table_ref[other, 0, at["up"] + way * bucket + i]] += beside_ref[way, i]
+        add(0, jnp.where(valid, how_many(table_ref[other, 0, LANES - 1], 1 + way), 0),
+            lambda i: table_ref[other, 0, at["up"] + way * bucket + i], lambda i: beside_ref[way, i])
 
     for way in range(2):
         for distance in range(1, reach + 1):
             source = ring_tile(tiles, tile, -distance if way == 0 else distance)
             reaches = reaching(tiles, bucket, way, lambda i: table_ref[source, 0, i])
-            start = own_rows + plan_ref[0, 1 + way * reach + distance - 1]
-
-            @pl.loop(reaches[distance + 1], reaches[distance])
-            def _(i):
-                out_ref[table_ref[source, 0, way * own_rows + i]] += pool_ref[way, start + i]
+            start = own_rows + table_ref[tiles + bands, 0, way * reach + distance - 1]
+            add(reaches[distance + 1], reaches[distance],
+                lambda i: table_ref[source, 0, way * own_rows + i], lambda i: pool_ref[way, start + i])
 
 
 def adaptive(tiles, bands, patches, pair_patch, pair_atm, numerators, counts):
@@ -636,15 +653,15 @@
     block = (cell_rows, flux)
     f32 = jnp.float32
     numerators = jnp.transpose(numerators, (0, 2, 1))
-    pool, beside, own, table, plan = pl.pallas_call(
+    pool, beside, own, table, flag = pl.pallas_call(
         functools.partial(stream_kernel, tiles, bands, bucket, blocks_owned, plans, group),
         out_shape=(jax.ShapeDtypeStruct((2, 2 * bucket + slots) + block, f32),
                    jax.ShapeDtypeStruct((2, bucket) + block, f32),
                    jax.ShapeDtypeStruct((bucket,) + block, f32),
-                   jax.ShapeDtypeStruct((tiles + bands, 1, LANES), jnp.int32),
-                   jax.ShapeDtypeStruct((1, LANES), jnp.int32)),
+                   jax.ShapeDtypeStruct((tiles + bands + 1, 1, LANES), jnp.int32),
+                   jax.ShapeDtypeStruct((1,), jnp.int32)),
         in_specs=[smem, smem, vmem, hbm, hbm],
-        out_specs=(vmem, vmem, vmem, smem, smem),
+        out_specs=(vmem, vmem, vmem, vmem, smem),
         scratch_shapes=[
             pltpu.VMEM((patches.shape[0] // patch_rows, patch_rows, flux), patches.dtype),
             pltpu.VMEM(numerators.shape, numerators.dtype),
@@ -656,8 +673,7 @@
             pltpu.VMEM((2, bucket) + block, f32),
             pltpu.VMEM((2, slots) + block, f32),
             pltpu.VMEM((2, slots) + block, f32),
-            pltpu.VMEM((tiles, 1, LANES), jnp.int32),
-            pltpu.VMEM((bands, 1, LANES), jnp.int32),
+            pltpu.SMEM((tiles + bands, 1, LANES), jnp.int32),
             pltpu.VMEM((1, LANES), jnp.int32),
             pltpu.SemaphoreType.DMA((2, most)),
             pltpu.SemaphoreType.DMA((2, most)),
@@ -671,22 +687,22 @@
         name="stream",
     )(pair_patch, counts, pair_atm.reshape(1, pairs), patches.reshape(-1, patch_rows, flux), numerators)
 
-    def take(patches, pair_patch, pair_atm, numerators, counts, table, plan, own, pool, beside):
+    def take(patches, pair_patch, pair_atm, numerators, counts, table, own, pool, beside):
         out = pl.pallas_call(
             functools.partial(take_kernel, tiles, bands, bucket),
             out_shape=jax.ShapeDtypeStruct((blocks_owned,) + block, f32),
-            in_specs=[smem, smem, vmem, vmem, vmem],
+            in_specs=[smem, vmem, vmem, vmem],
             out_specs=vmem,
             compiler_params=pltpu.CompilerParams(vmem_limit_bytes=VMEM_LIMIT),
             name="take",
-        )(table, plan, own, pool, beside)
+        )(table, own, pool, beside)
         return out.reshape(blocks_owned * cell_rows, flux)
 
-    def padded(patches, pair_patch, pair_atm, numerators, counts, table, plan, own, pool, beside):
+    def padded(patches, pair_patch, pair_atm, numerators, counts, table, own, pool, beside):
         return per_device(tiles, bands, patches, pair_patch, pair_atm, numerators, counts)
 
-    return lax.cond(plan[0, 0] > 0, padded, take, patches, pair_patch, pair_atm, numerators, counts,
-                    table, plan, own, pool, beside)
+    return lax.cond(flag[0] > 0, padded, take, patches, pair_patch, pair_atm, numerators, counts,
+                    table, own, pool, beside)
 
 
 def solution(mesh):

time: 37.2 us -> 36.8 us (0.989)
  Pallas kernels: 36.4 us -> 35.2 us
  between operations: 0.73 us -> 1.32 us
    pallas_call x1, Pallas kernels: 33.6 us -> 32.7 us  [adaptive(): pl.pallas_call(functools.partial(stream_kernel, tiles, bands, bucket, blo...]
where the time goes in v2:
time: 36.8 us; the launch traced here: 36.6 us
  Pallas kernels  35.2 us (96%)
  between operations  1.32 us (4%)
    pallas_call x1, Pallas kernels, adaptive(): pl.pallas_call(functools.partial(stream_kernel, tiles, bands, bucket, blo...  32.7 us
    pallas_call x1, Pallas kernels, take(): pl.pallas_call(functools.partial(take_kernel, tiles, bands, bucket), out_...  2.53 us

profile of v2, /device:TPU:0, one launch (start us, length us, event | category | flops | bytes accessed | tf_op | source)
XLA Modules:
  0.0 36.6 jit_solution(10376253928226656741)
XLA Ops:
  0.7 0.0 copy-start.2
  0.7 0.0 copy-start.3
  0.7 32.7 %stream.1 = (f32[2,112,32,128]{3,2,1,0:T(8,128)S(1)}, f32[2,16,32,128]{3,2,1,0:T(8,128)S(1)}, f32[16,32,128]{2,1,0:T(8,128)S(1)}, s32[13,1,128]{2,1,0:T(1,128)S(1)}, s32[1]{0:T(128)}) custom-call(s32[128]{0:T(128)} %patch_ref.1, s32[1]{0:T(128)S(6)} %copy.10.counts_ref, s32[1,128]{1,0:T(1,128)} %bitcast.9, bf16[64,128,128]{2,1,0:T(8,128)(2,1)} %bitcast.6, ...), custom_call_target="tpu_custom_call" | custom-call | tf_op jit(solution)/shard_map/stream/pallas_call | solution.py:656
  34.0 0.0 copy-done.2
  34.0 0.0 copy-done.3
  34.0 2.5 %conditional.1 = (f32[4096,128]{1,0:T(8,128)}) conditional(s32[]{:T(128)} %bitcast.5, (s32[13,1,128]{2,1,0:T(1,128)S(1)}, f32[16,32,128]{2,1,0:T(8,128)S(1)}, f32[2,112,32,128]{3,2,1,0:T(8,128)S(1)}, f32[2,16,32,128]{3,2,1,0:T(8,128)S(1)}) %tuple.11, (s32[128]{0:T(128)S(1)}, s32[128]{0:T(128)S(1)}, s32[1]{0:T(128)}, bf16[8192,128]{1,0:T(8,128)(2,1)}, ...), branch_computations={%region_0.0_spmd, %region_1.0_spmd} | conditional | bytes 10571840 | solution.py:704
  34.0 2.5 %take.1 = f32[128,32,128]{2,1,0:T(8,128)} custom-call(s32[13,1,128]{2,1,0:T(1,128)S(1)} %get-tuple-element.26.table_ref, f32[16,32,128]{2,1,0:T(8,128)S(1)} %get-tuple-element.27.own_ref, f32[2,112,32,128]{3,2,1,0:T(8,128)S(1)} %get-tuple-element.28.pool_ref, f32[2,16,32,128]{3,2,1,0:T(8,128)S(1)} %get-tuple-element.29.beside_ref), custom_call_target="tpu_custom_call" | custom-call | tf_op jit(solution)/shard_map/cond/branch_0_fun/take/pallas_call | solution.py:691
Async XLA Ops:
  0.7 33.4 %copy-start.2 = (s32[128]{0:T(128)S(1)}, s32[128]{0:T(128)}, u32[]{:S(2)}) copy-start(s32[128]{0:T(128)} %patch_ref.1) | copy-start | bytes 1540
  0.7 33.4 %copy-start.3 = (s32[128]{0:T(128)S(1)}, s32[128]{0:T(128)}, u32[]{:S(2)}) copy-start(s32[128]{0:T(128)} %param.9) | copy-start | bytes 1540

commit v3 on v2

--- a/solution.py
+++ b/solution.py
@@ -345,14 +345,24 @@
     fits = place < room
     slot = jnp.where((one_lane < live) & fits, base + place, pairs)
     overflow = jnp.max(jnp.where((one_lane < live) & jnp.logical_not(fits), 1, 0), axis=1, keepdims=True)
+    travels_c = live_c & (b_c > 0) & (b_c < tiles)
+    travelling = count(travels_c)
+    earlier = count(travels_c & (row < lane))
+    rank_of = jnp.where((one_lane < live) & ring, earlier, travelling + one_lane - earlier)
+    rank_c = across(rank_of)
+    overflow = jnp.maximum(overflow, jnp.where(travelling > pairs // 2, 1, 0))
+    here_c = rank_c == lane
+    pair_at = most(jnp.where(here_c, row, 0))
+    before = most(jnp.where(row == before, rank_c, -1))
+    before = most(jnp.where(here_c, across(before), -1))
     hit = across(slot) == lane
-    last = most(jnp.where(hit, row, 0))
+    last = most(jnp.where(hit, rank_c, 0))
     label = most(jnp.where(hit, block_c, -1))
     counts = count(fresh_c & (b_c == lane - (7 * bucket - 1)))
     kinds = [count(fresh_c & (b_c == k)) for k in (0, tiles, tiles + 1)]
     packed = overflow + sum(kind << (1 + 6 * i) for i, kind in enumerate(kinds))
     labels = jnp.where(one_lane < 7 * bucket, label, jnp.where(one_lane == pairs - 1, packed, counts))
-    return before, last, labels
+    return before, last, pair_at, labels
 
 
 def starts(reach, lag, reaches):
@@ -395,26 +405,30 @@
         pl.semaphore_signal(barrier, inc=1, device_id=(band, step(tile)), device_id_type=MESH)
     for j in range(1, bands):
         pl.semaphore_signal(barrier, inc=1, device_id=(lax.rem(band + j, bands), tile), device_id_type=MESH)
-    before, last, labels = sort_pairs(tiles, bands, bucket, blocks_owned, band, tile, counts_ref[0], atm_ref[...])
+    before, last, pair_at, labels = sort_pairs(tiles, bands, bucket, blocks_owned, band, tile, counts_ref[0], atm_ref[...])
     labels_ref[...] = labels
     landing[tile] = labels
     work_v[0:1] = before
     work_v[1:2] = last
+    work_v[2:3] = pair_at
     work_in = pltpu.make_async_copy(work_v, work_ref, local_sem)
     work_in.start()
     work_in.wait()
     patch_load.wait()
-
-    @pl.loop(0, pairs // group)
-    def _(c):
+    for c in range(pairs // group):
         numer_load(c).wait()
+
+    def multiply(c):
         for j in range(group):
-            g = c * group + j
+            k = c * group + j
+            g = work_ref[2, k]
             weight = (numer_ref[g].astype(jnp.float32) * SCALE).astype(jnp.bfloat16)
             part = jnp.dot(weight, patches_ref[patch_ref[g]], preferred_element_type=jnp.float32)
-            before = work_ref[0, g]
+            before = work_ref[0, k]
             earlier = sums[jnp.maximum(before, 0)]
-            sums[g] = part + jnp.where(before >= 0, earlier, 0.0)
+            sums[k] = part + jnp.where(before >= 0, earlier, 0.0)
+
+    pl.loop(0, pairs // group // 2)(multiply)
 
     def total(slot):
         return sums[work_ref[1, slot]]
@@ -472,6 +486,7 @@
             device_id=(target_band, tile), device_id_type=MESH)
 
     upward, downward = beside(0, band + 1), beside(1, band - 1)
+    pl.loop(pairs // group // 2, pairs // group)(multiply)
     for way in range(2):
         for s in range(bucket):
             side[way, s] = total(at["up"] + way * bucket + s)
@@ -566,7 +581,7 @@
     rows_over.wait()
     for j in range(1, bands):
         flag = jnp.maximum(flag, table_ref[tiles + lax.rem(band + j, bands), 0, LANES - 1] & 1)
-    flag_ref[0] = flag
+    flag_ref[0, 0] = flag
 
     @pl.when(band < bands - 1)
     def _():
@@ -659,15 +674,15 @@
                    jax.ShapeDtypeStruct((2, bucket) + block, f32),
                    jax.ShapeDtypeStruct((bucket,) + block, f32),
                    jax.ShapeDtypeStruct((tiles + bands + 1, 1, LANES), jnp.int32),
-                   jax.ShapeDtypeStruct((1,), jnp.int32)),
+                   jax.ShapeDtypeStruct((1, LANES), jnp.int32)),
         in_specs=[smem, smem, vmem, hbm, hbm],
         out_specs=(vmem, vmem, vmem, vmem, smem),
         scratch_shapes=[
             pltpu.VMEM((patches.shape[0] // patch_rows, patch_rows, flux), patches.dtype),
             pltpu.VMEM(numerators.shape, numerators.dtype),
             pltpu.VMEM((1, LANES), jnp.int32),
-            pltpu.VMEM((2, pairs), jnp.int32),
-            pltpu.SMEM((2, pairs), jnp.int32),
+            pltpu.VMEM((3, pairs), jnp.int32),
+            pltpu.SMEM((3, pairs), jnp.int32),
             pltpu.SemaphoreType.DMA((pairs // group + 1,)),
             pltpu.VMEM((pairs,) + block, f32),
             pltpu.VMEM((2, bucket) + block, f32),
@@ -701,7 +716,7 @@
     def padded(patches, pair_patch, pair_atm, numerators, counts, table, own, pool, beside):
         return per_device(tiles, bands, patches, pair_patch, pair_atm, numerators, counts)
 
-    return lax.cond(flag[0] > 0, padded, take, patches, pair_patch, pair_atm, numerators, counts,
+    return lax.cond(flag[0, 0] > 0, padded, take, patches, pair_patch, pair_atm, numerators, counts,
                     table, own, pool, beside)
 
 

time: 36.8 us -> 35.8 us (0.973)
  between operations: 1.32 us -> 0.73 us
  Pallas kernels: 35.2 us -> 34.8 us
    pallas_call x1, Pallas kernels: 32.7 us -> 32.3 us  [adaptive(): pl.pallas_call(functools.partial(stream_kernel, tiles, bands, bucket, blo...]
where the time goes in v3:
time: 35.8 us; the launch traced here: 35.5 us
  Pallas kernels  34.8 us (97%)
  between operations  0.73 us (2%)
    pallas_call x1, Pallas kernels, adaptive(): pl.pallas_call(functools.partial(stream_kernel, tiles, bands, bucket, blo...  32.3 us
    pallas_call x1, Pallas kernels, take(): pl.pallas_call(functools.partial(take_kernel, tiles, bands, bucket), out_...  2.53 us

profile of v3, /device:TPU:0, one launch (start us, length us, event | category | flops | bytes accessed | tf_op | source)
XLA Modules:
  0.0 35.5 jit_solution(9706379585415888817)
XLA Ops:
  0.7 0.0 copy-start.2
  0.7 0.0 copy-start.3
  0.7 32.3 %stream.1 = (f32[2,112,32,128]{3,2,1,0:T(8,128)S(1)}, f32[2,16,32,128]{3,2,1,0:T(8,128)S(1)}, f32[16,32,128]{2,1,0:T(8,128)S(1)}, s32[13,1,128]{2,1,0:T(1,128)S(1)}, s32[1,128]{1,0:T(1,128)S(1)}) custom-call(s32[128]{0:T(128)} %patch_ref.1, s32[1]{0:T(128)S(6)} %copy.10.counts_ref, s32[1,128]{1,0:T(1,128)} %bitcast.11, bf16[64,128,128]{2,1,0:T(8,128)(2,1)} %bitcast.8, ...), custom_call_target="tpu_custom_call" | custom-call | tf_op jit(solution)/shard_map/stream/pallas_call | solution.py:671
  33.0 0.0 copy-done.2
  33.0 0.0 copy-done.3
  33.0 2.5 %conditional.1 = (f32[4096,128]{1,0:T(8,128)}) conditional(s32[]{:T(128)} %bitcast.5, (s32[13,1,128]{2,1,0:T(1,128)S(1)}, f32[16,32,128]{2,1,0:T(8,128)S(1)}, f32[2,112,32,128]{3,2,1,0:T(8,128)S(1)}, f32[2,16,32,128]{3,2,1,0:T(8,128)S(1)}) %tuple.11, (s32[128]{0:T(128)S(1)}, s32[128]{0:T(128)S(1)}, s32[1]{0:T(128)}, bf16[8192,128]{1,0:T(8,128)(2,1)}, ...), branch_computations={%region_0.0_spmd, %region_1.0_spmd} | conditional | bytes 10571840 | solution.py:719
  33.0 2.5 %take.1 = f32[128,32,128]{2,1,0:T(8,128)} custom-call(s32[13,1,128]{2,1,0:T(1,128)S(1)} %get-tuple-element.26.table_ref, f32[16,32,128]{2,1,0:T(8,128)S(1)} %get-tuple-element.27.own_ref, f32[2,112,32,128]{3,2,1,0:T(8,128)S(1)} %get-tuple-element.28.pool_ref, f32[2,16,32,128]{3,2,1,0:T(8,128)S(1)} %get-tuple-element.29.beside_ref), custom_call_target="tpu_custom_call" | custom-call | tf_op jit(solution)/shard_map/cond/branch_0_fun/take/pallas_call | solution.py:706
Async XLA Ops:
  0.7 32.3 %copy-start.2 = (s32[128]{0:T(128)S(1)}, s32[128]{0:T(128)}, u32[]{:S(2)}) copy-start(s32[128]{0:T(128)} %patch_ref.1) | copy-start | bytes 1540
  0.7 32.3 %copy-start.3 = (s32[128]{0:T(128)S(1)}, s32[128]{0:T(128)}, u32[]{:S(2)}) copy-start(s32[128]{0:T(128)} %param.9) | copy-start | bytes 1540

commit v4 on v3

--- a/solution.py
+++ b/solution.py
@@ -659,7 +659,7 @@
     bucket = pairs // 8
     reach = tiles // 2
     group = 16
-    plans = ((5, 4 * reach, 4), (3, 4 * reach, 3))
+    plans = ((5, 4 * reach + 1, 4), (3, 4 * reach + 1, 3))
     slots = max(size * rounds for size, rounds, _ in plans)
     most = max(rounds for _, rounds, _ in plans)
     smem = pl.BlockSpec(memory_space=pltpu.SMEM)

time: 35.8 us -> 37.2 us (1.039)
  Pallas kernels: 34.8 us -> 36.3 us
    pallas_call x1, Pallas kernels: 32.3 us -> 33.7 us  [adaptive(): pl.pallas_call(functools.partial(stream_kernel, tiles, bands, bucket, blo...]
where the time goes in v4:
time: 37.2 us; the launch traced here: 37 us
  Pallas kernels  36.3 us (98%)
  between operations  0.73 us (2%)
    pallas_call x1, Pallas kernels, adaptive(): pl.pallas_call(functools.partial(stream_kernel, tiles, bands, bucket, blo...  33.7 us
    pallas_call x1, Pallas kernels, take(): pl.pallas_call(functools.partial(take_kernel, tiles, bands, bucket), out_...  2.57 us

profile of v4, /device:TPU:0, one launch (start us, length us, event | category | flops | bytes accessed | tf_op | source)
XLA Modules:
  0.0 37.0 jit_solution(1290714178134232937)
XLA Ops:
  0.7 0.0 copy-start.2
  0.7 0.0 copy-start.3
  0.7 33.7 %stream.1 = (f32[2,117,32,128]{3,2,1,0:T(8,128)S(1)}, f32[2,16,32,128]{3,2,1,0:T(8,128)S(1)}, f32[16,32,128]{2,1,0:T(8,128)S(1)}, s32[13,1,128]{2,1,0:T(1,128)S(1)}, s32[1,128]{1,0:T(1,128)S(1)}) custom-call(s32[128]{0:T(128)} %patch_ref.1, s32[1]{0:T(128)S(6)} %copy.10.counts_ref, s32[1,128]{1,0:T(1,128)} %bitcast.11, bf16[64,128,128]{2,1,0:T(8,128)(2,1)} %bitcast.8, ...), custom_call_target="tpu_custom_call" | custom-call | tf_op jit(solution)/shard_map/stream/pallas_call | solution.py:671
  34.4 0.0 copy-done.2
  34.4 0.0 copy-done.3
  34.4 2.6 %conditional.1 = (f32[4096,128]{1,0:T(8,128)}) conditional(s32[]{:T(128)} %bitcast.5, (s32[13,1,128]{2,1,0:T(1,128)S(1)}, f32[16,32,128]{2,1,0:T(8,128)S(1)}, f32[2,117,32,128]{3,2,1,0:T(8,128)S(1)}, f32[2,16,32,128]{3,2,1,0:T(8,128)S(1)}) %tuple.11, (s32[128]{0:T(128)S(1)}, s32[128]{0:T(128)S(1)}, s32[1]{0:T(128)}, bf16[8192,128]{1,0:T(8,128)(2,1)}, ...), branch_computations={%region_0.0_spmd, %region_1.0_spmd} | conditional | bytes 10571840 | solution.py:719
  34.4 2.6 %take.1 = f32[128,32,128]{2,1,0:T(8,128)} custom-call(s32[13,1,128]{2,1,0:T(1,128)S(1)} %get-tuple-element.26.table_ref, f32[16,32,128]{2,1,0:T(8,128)S(1)} %get-tuple-element.27.own_ref, f32[2,117,32,128]{3,2,1,0:T(8,128)S(1)} %get-tuple-element.28.pool_ref, f32[2,16,32,128]{3,2,1,0:T(8,128)S(1)} %get-tuple-element.29.beside_ref), custom_call_target="tpu_custom_call" | custom-call | tf_op jit(solution)/shard_map/cond/branch_0_fun/take/pallas_call | solution.py:706
Async XLA Ops:
  0.7 33.8 %copy-start.2 = (s32[128]{0:T(128)S(1)}, s32[128]{0:T(128)}, u32[]{:S(2)}) copy-start(s32[128]{0:T(128)} %patch_ref.1) | copy-start | bytes 1540
  0.7 33.8 %copy-start.3 = (s32[128]{0:T(128)S(1)}, s32[128]{0:T(128)}, u32[]{:S(2)}) copy-start(s32[128]{0:T(128)} %param.9) | copy-start | bytes 1540

commit v5 on v4

--- a/solution.py
+++ b/solution.py
@@ -658,8 +658,8 @@
     blocks_owned = CELLS_DEV // cell_rows
     bucket = pairs // 8
     reach = tiles // 2
-    group = 16
-    plans = ((5, 4 * reach + 1, 4), (3, 4 * reach + 1, 3))
+    group = 32
+    plans = ((4, 5 * reach, 5), (3, 4 * reach, 3))
     slots = max(size * rounds for size, rounds, _ in plans)
     most = max(rounds for _, rounds, _ in plans)
     smem = pl.BlockSpec(memory_space=pltpu.SMEM)

time: 37.2 us -> 35.6 us (0.957)
  Pallas kernels: 36.3 us -> 34.7 us
    pallas_call x1, Pallas kernels: 33.7 us -> 32 us  [adaptive(): pl.pallas_call(functools.partial(stream_kernel, tiles, bands, bucket, blo...]
where the time goes in v5:
time: 35.6 us; the launch traced here: 35.4 us
  Pallas kernels  34.7 us (97%)
  between operations  0.73 us (2%)
    pallas_call x1, Pallas kernels, adaptive(): pl.pallas_call(functools.partial(stream_kernel, tiles, bands, bucket, blo...  32 us
    pallas_call x1, Pallas kernels, take(): pl.pallas_call(functools.partial(take_kernel, tiles, bands, bucket), out_...  2.64 us

profile of v5, /device:TPU:0, one launch (start us, length us, event | category | flops | bytes accessed | tf_op | source)
XLA Modules:
  0.0 35.4 jit_solution(6961106742690775139)
XLA Ops:
  0.7 0.0 copy-start.2
  0.7 0.0 copy-start.3
  0.7 32.0 %stream.1 = (f32[2,112,32,128]{3,2,1,0:T(8,128)S(1)}, f32[2,16,32,128]{3,2,1,0:T(8,128)S(1)}, f32[16,32,128]{2,1,0:T(8,128)S(1)}, s32[13,1,128]{2,1,0:T(1,128)S(1)}, s32[1,128]{1,0:T(1,128)S(1)}) custom-call(s32[128]{0:T(128)} %patch_ref.1, s32[1]{0:T(128)S(6)} %copy.10.counts_ref, s32[1,128]{1,0:T(1,128)} %bitcast.11, bf16[64,128,128]{2,1,0:T(8,128)(2,1)} %bitcast.8, ...), custom_call_target="tpu_custom_call" | custom-call | tf_op jit(solution)/shard_map/stream/pallas_call | solution.py:671
  32.8 0.0 copy-done.2
  32.8 0.0 copy-done.3
  32.8 2.7 %conditional.1 = (f32[4096,128]{1,0:T(8,128)}) conditional(s32[]{:T(128)} %bitcast.5, (s32[13,1,128]{2,1,0:T(1,128)S(1)}, f32[16,32,128]{2,1,0:T(8,128)S(1)}, f32[2,112,32,128]{3,2,1,0:T(8,128)S(1)}, f32[2,16,32,128]{3,2,1,0:T(8,128)S(1)}) %tuple.11, (s32[128]{0:T(128)S(1)}, s32[128]{0:T(128)S(1)}, s32[1]{0:T(128)}, bf16[8192,128]{1,0:T(8,128)(2,1)}, ...), branch_computations={%region_0.0_spmd, %region_1.0_spmd} | conditional | bytes 10571840 | solution.py:719
  32.8 2.6 %take.1 = f32[128,32,128]{2,1,0:T(8,128)} custom-call(s32[13,1,128]{2,1,0:T(1,128)S(1)} %get-tuple-element.26.table_ref, f32[16,32,128]{2,1,0:T(8,128)S(1)} %get-tuple-element.27.own_ref, f32[2,112,32,128]{3,2,1,0:T(8,128)S(1)} %get-tuple-element.28.pool_ref, f32[2,16,32,128]{3,2,1,0:T(8,128)S(1)} %get-tuple-element.29.beside_ref), custom_call_target="tpu_custom_call" | custom-call | tf_op jit(solution)/shard_map/cond/branch_0_fun/take/pallas_call | solution.py:706
Async XLA Ops:
  0.7 32.1 %copy-start.2 = (s32[128]{0:T(128)S(1)}, s32[128]{0:T(128)}, u32[]{:S(2)}) copy-start(s32[128]{0:T(128)} %patch_ref.1) | copy-start | bytes 1540
  0.7 32.1 %copy-start.3 = (s32[128]{0:T(128)S(1)}, s32[128]{0:T(128)}, u32[]{:S(2)}) copy-start(s32[128]{0:T(128)} %param.9) | copy-start | bytes 1540
